TPU v7x, 512 devices: a whole 4x8x8 slice. The times are simulated.
512 devices in a mesh: slab: 64 (over z, x, core), tile: 8 (over y).
Axes of the slice: x: 4, y: 8, z: 8, core: 2. Of those that a mesh axis runs over, the one named last changes fastest.
Arguments:
- features: bfloat16 [64, 8, 512, 128], P('slab', 'tile'), may hold values from -24 to 24
- counts: int32 [64, 8], P('slab', 'tile'), may hold values from 128 to 512, as said below
- rulebook: int32 [64, 8, 27, 512], P('slab', 'tile'), may hold values from 0 to 800, as said below
- face_rows: int32 [64, 8, 4, 64], P('slab', 'tile'), may hold values from 0 to 511, as said below
- conv_one: bfloat16 [27, 128, 128], replicated, may hold values from -0.109375 to 0.109375
- gain_one: float32 [128], replicated, may hold values from 0.5 to 1.5
- shift_one: float32 [128], replicated, may hold values from -0.5 to 0.5
- conv_two: bfloat16 [27, 128, 128], replicated, may hold values from -0.109375 to 0.109375
- gain_two: float32 [128], replicated, may hold values from 0.5 to 1.5
- shift_two: float32 [128], replicated, may hold values from -0.5 to 0.5
Outputs:
- output: bfloat16 [64, 8, 512, 128], P('slab', 'tile')
Inputs may be any that keep to these rules, and one draw needn't show every extreme that they name: `counts`: each device's voxels fill its 8 x 8 grid columns with the same number each, between 2 and 8; some device of the highest slab index holds 512. `rulebook`: an entry names the extended-table row that holds the voxel's neighbour at offset k = 9 (dx + 1) + 3 (dy + 1) + (dz + 1) of the submanifold 3x3x3 stencil, or 800 where that cell is inactive or outside the grid; the voxel itself is at offset 13; rows at or past the device's count name 800 at every offset. `face_rows`: lists 0 to 3 hold the device's voxels on its lower and higher face along the first, then the lower and higher face along the second dimension; the j-th voxel of the i-th column along a face stands at position i * 8 + j; unused positions name row 0.
All inputs are finite; a program needn't handle non-finite values.
Results may differ from a plain program's by a relative error of at most 0.0033.
Values may be sent and summed in bfloat16 or wider, within the bound.
No kernel may reach another device: no remote copies, remote signals or barrier semaphores. Data moves between devices by JAX's collectives and lax.ppermute only.
A program may use at most 64 MiB of HBM per device.

v0:
```python
from functools import partial
import jax
import jax.numpy as jnp
from jax import lax
from jax.sharding import Mesh
from jax.sharding import PartitionSpec as P

SIDE = 8
SLAB = ("slab_0", "slab_1", "slab_2")
SLAB_TILE = ("slab_0", "slab_1", "slab_2", "tile")
EPSILON = 1e-05


def extended(block, sides, width):
    for axis, dim in sides:
        count = lax.axis_size(axis)
        forward = [(i, i + 1) for i in range(count - 1)]
        backward = [(target, source) for source, target in forward]
        low = lax.ppermute(
            lax.slice_in_dim(block, block.shape[dim] - width, None, axis=dim), axis, forward
        )
        high = lax.ppermute(lax.slice_in_dim(block, 0, width, axis=dim), axis, backward)
        block = jnp.concatenate([low, block, high], axis=dim)
    return block


def by_axis(shard, axes):
    for axis in axes:
        shard = lax.psum(shard, axis)
    return shard


def build_table(local_rows, face_lists):
    face_len = face_lists.shape[1]
    column = face_len // SIDE
    picked = local_rows[face_lists]
    tile_recv = extended(picked[2:4], (("tile", 0),), 1)
    core_low = tile_recv[0]
    core_high = tile_recv[3]
    slab_send = jnp.stack(
        [
            jnp.concatenate([picked[0], core_low[:column], core_high[:column]], axis=0),
            jnp.concatenate(
                [picked[1], core_low[face_len - column :], core_high[face_len - column :]], axis=0
            ),
        ]
    )
    slab_recv = extended(slab_send, ((SLAB, 0),), 1)
    low_full = slab_recv[0]
    high_full = slab_recv[3]
    slab_low = low_full[:face_len]
    slab_high = high_full[:face_len]
    tile_low = jnp.concatenate(
        [low_full[face_len : face_len + column], core_low, high_full[face_len : face_len + column]],
        axis=0,
    )
    tile_high = jnp.concatenate(
        [low_full[face_len + column :], core_high, high_full[face_len + column :]], axis=0
    )
    zero_row = jnp.zeros((1, local_rows.shape[1]), local_rows.dtype)
    return jnp.concatenate([local_rows, slab_low, slab_high, tile_low, tile_high, zero_row], axis=0)


def pick_rows(lookup, tap_index, offset, block_rows, flat_weight):
    gathered = jnp.take(lookup, tap_index.T, axis=0)
    gathered = gathered.reshape(block_rows, tap_index.shape[0] * lookup.shape[1])
    return jnp.dot(gathered, flat_weight, preferred_element_type=jnp.float32)


def convolve(lookup, tap_index, weight):
    total_rows = tap_index.shape[1]
    block_rows = min(512, total_rows)
    flat_weight = weight.reshape(weight.shape[0] * weight.shape[1], weight.shape[2])
    compute = partial(pick_rows, lookup, tap_index, 0, block_rows, flat_weight)
    result = compute()
    return result


def normalize(conv_out, live_mask, count_value, gain, shift):
    first_sum = jnp.sum(conv_out * live_mask, axis=0)
    square_sum = jnp.sum(conv_out * conv_out * live_mask, axis=0)
    channel_sums, square_sums, voxel_total = (
        by_axis(first_sum, SLAB_TILE),
        by_axis(square_sum, SLAB_TILE),
        by_axis(count_value, SLAB_TILE),
    )
    average = channel_sums / voxel_total
    variance = square_sums / voxel_total - average * average
    return (conv_out - average) * lax.rsqrt(variance + EPSILON) * gain + shift


def per_device(
    features,
    counts,
    rulebook,
    face_rows,
    conv_one,
    gain_one,
    shift_one,
    conv_two,
    gain_two,
    shift_two,
):
    local_rows = features[0, 0]
    face_lists = face_rows[0, 0]
    tap_index = rulebook[0, 0]
    voxel_count = counts[0, 0]
    count_value = voxel_count.astype(jnp.float32)
    live_mask = (lax.broadcasted_iota(jnp.int32, (local_rows.shape[0], 1), 0) < voxel_count).astype(
        jnp.float32
    )
    first = convolve(build_table(local_rows, face_lists), tap_index, conv_one)
    hidden = (
        live_mask * jnp.maximum(normalize(first, live_mask, count_value, gain_one, shift_one), 0.0)
    ).astype(jnp.bfloat16)
    second = convolve(build_table(hidden, face_lists), tap_index, conv_two)
    summed = normalize(second, live_mask, count_value, gain_two, shift_two) + local_rows.astype(
        jnp.float32
    )
    output = (live_mask * jnp.maximum(summed, 0.0)).astype(jnp.bfloat16)
    return output[None, None]


def solution(mesh):
    torus = Mesh(
        mesh.devices.reshape(8, 4, 2, mesh.shape["tile"]), ("slab_0", "slab_1", "slab_2", "tile")
    )
    in_specs = (
        P(SLAB, "tile", None, None),
        P(SLAB, "tile"),
        P(SLAB, "tile", None, None),
        P(SLAB, "tile", None, None),
        P(),
        P(),
        P(),
        P(),
        P(),
        P(),
    )
    out_specs = P(SLAB, "tile", None, None)
    return jax.shard_map(
        per_device, mesh=torus, in_specs=in_specs, out_specs=out_specs, check_vma=False
    )
```

profile of v0, /device:TPU:2, one launch (start us, length us, event | category | flops | bytes accessed | tf_op | source)
XLA Modules:
  0.0 231.2 jit_solution(8170010614980495106)
XLA Ops:
  0.0 0.0 copy-start
  0.0 0.8 compare_select_fusion.1
  0.8 0.1 reshape.90
  0.9 1.6 gather_fusion
  2.5 3.5 %collective-permute-start = (bf16[1,64,128]{2,1,0:T(8,128)(2,1)S(1)}, bf16[1,64,128]{2,1,0:T(8,128)(2,1)S(1)}, u32[]{:S(2)}, u32[]{:S(2)}) collective-permute-start(bf16[1,64,128]{2,1,0:T(8,128)(2,1)S(1)} %get-tuple-element.42), channel_id=1, source_target_pairs={{0,1},{1,2},{2,3},{3,4},{4,5},{5,6},{6,7},{8,9},{9,10},{10,11},{11... | collective-permute-start | bytes 49160 | tf_op jit(solution)/shard_map/ppermute | solution.py:19
  6.0 1.3 collective-permute-start.1
  7.3 0.9 constant_dynamic-update-slice_fusion.9
  8.2 0.8 compare_select_fusion
  9.1 0.8 compare_and_fusion
  9.9 0.1 copy.15
  10.0 0.2 reshape.122
  10.9 0.2 copy.13
  11.1 0.0 collective-permute-done
  11.1 0.5 collective-permute-done.1
  11.6 1.9 collective-permute-start.2
  13.6 3.6 %collective-permute-start.3 = (bf16[1,80,128]{2,1,0:T(8,128)(2,1)S(1)}, bf16[1,80,128]{2,1,0:T(8,128)(2,1)S(1)}, u32[]{:S(2)}, u32[]{:S(2)}) collective-permute-start(bf16[1,80,128]{2,1,0:T(8,128)(2,1)S(1)} %maximum_bitcast_fusion.1), channel_id=1, source_target_pairs={{8,0},{16,8},{24,16},{32,24},{40,32},{48,40},{56,48},{64,56},{72,6... | collective-permute-start | bytes 61448 | tf_op jit(solution)/shard_map/ppermute | solution.py:22
  17.2 0.0 collective-permute-done.2
  17.2 1.4 collective-permute-done.3
  18.8 28.4 %gather_fusion.2 = bf16[13824,128]{1,0:T(8,128)(2,1)} fusion(bf16[801,128]{1,0:T(8,128)(2,1)S(1)} %constant_dynamic-update-slice_fusion, s32[14336]{0:T(1024)S(1)} %pad_clamp_fusion), kind=kCustom, calls=%fused_computation.clone | custom fusion | bytes 7133184 | tf_op jit(solution)/shard_map/jit(_take)/gather | solution.py:65
  47.1 6.6 %reshape.125 = bf16[512,27,128]{2,1,0:T(8,128)(2,1)} reshape(bf16[13824,128]{1,0:T(8,128)(2,1)} %gather_fusion.2) | data formatting | bytes 7077888 | tf_op jit(solution)/shard_map/jit(_take)/gather | solution.py:65
  53.7 10.1 %broadcast_select_fusion = bf16[512,27,128]{2,1,0:T(8,128)(2,1)S(1)} fusion(bf16[512,27,128]{2,1,0:T(8,128)(2,1)} %reshape.125, pred[512,27]{1,0:T(8,128)(4,1)S(1)} %copy.13), kind=kLoop, calls=%fused_computation.4 | loop fusion | flops 1769472 | bytes 7091712 | tf_op jit(solution)/shard_map/jit(_take)/select_n | solution.py:65
  63.8 0.0 copy-done
  63.8 0.0 copy-start.2
  63.8 0.0 copy-start.3
  63.8 1.3 multiply_reduce_fusion.2
  65.1 23.7 %all-reduce.3 = (f32[128]{0:T(128)S(1)}, f32[]{:T(128)}, f32[128]{0:T(128)S(1)}) all-reduce(f32[128]{0:T(128)S(1)} %get-tuple-element.9, f32[]{:T(128)S(6)} %convert_element_type.21, f32[128]{0:T(128)S(1)} %get-tuple-element.8), channel_id=1, replica_groups=mesh['slab_0'=8,'slab_1'=4,'slab_2'=2,'tile'=8] {'slab_0'}, use_global_device_ids=true, to_apply=%region_1.3 | all-reduce | flops 257 | bytes 2056 | tf_op jit(solution)/shard_map/psum | solution.py:29
  88.8 11.0 %all-reduce.5 = (f32[128]{0:T(128)S(1)}, f32[]{:T(128)}, f32[128]{0:T(128)S(1)}) all-reduce(f32[128]{0:T(128)S(1)} %get-tuple-element.17, f32[]{:T(128)} %get-tuple-element.18, f32[128]{0:T(128)S(1)} %get-tuple-element.19), channel_id=1, replica_groups=mesh['slab_0'=8,'slab_1'=4,'slab_2'=2,'tile'=8] {'slab_1'}, use_global_device_ids=true, to_apply=%region_2.4 | all-reduce | flops 257 | bytes 2056 | tf_op jit(solution)/shard_map/psum | solution.py:29
  99.8 3.1 %all-reduce.7 = (f32[128]{0:T(128)S(1)}, f32[]{:T(128)}, f32[128]{0:T(128)S(1)}) all-reduce(f32[128]{0:T(128)S(1)} %get-tuple-element.22, f32[]{:T(128)} %get-tuple-element.23, f32[128]{0:T(128)S(1)} %get-tuple-element.24), channel_id=1, replica_groups=mesh['slab_0'=8,'slab_1'=4,'slab_2'=2,'tile'=8] {'slab_2'}, use_global_device_ids=true, to_apply=%region_3.5 | all-reduce | flops 257 | bytes 2056 | tf_op jit(solution)/shard_map/psum | solution.py:29
  102.9 18.8 %all-reduce.1 = (f32[128]{0:T(128)S(1)}, f32[]{:T(128)}, f32[128]{0:T(128)S(1)}) all-reduce(f32[128]{0:T(128)S(1)} %get-tuple-element.27, f32[]{:T(128)} %get-tuple-element.28, f32[128]{0:T(128)S(1)} %get-tuple-element.29), channel_id=1, replica_groups=mesh['slab_0'=8,'slab_1'=4,'slab_2'=2,'tile'=8] {'tile'}, use_global_device_ids=true, to_apply=%region_4.6 | all-reduce | flops 257 | bytes 2056 | tf_op jit(solution)/shard_map/psum | solution.py:29
  121.7 0.7 add_rsqrt_fusion.1
  122.4 0.0 copy-done.2
  122.4 0.0 copy-done.3
  122.4 0.1 constant_dynamic-update-slice_fusion.19
  122.6 0.9 gather_fusion.1
  123.4 2.7 %collective-permute-start.4 = (bf16[1,64,128]{2,1,0:T(8,128)(2,1)S(1)}, bf16[1,64,128]{2,1,0:T(8,128)(2,1)S(1)}, u32[]{:S(2)}, u32[]{:S(2)}) collective-permute-start(bf16[1,64,128]{2,1,0:T(8,128)(2,1)S(1)} %get-tuple-element.38), channel_id=1, source_target_pairs={{0,1},{1,2},{2,3},{3,4},{4,5},{5,6},{6,7},{8,9},{9,10},{10,11},{11... | collective-permute-start | bytes 49160 | tf_op jit(solution)/shard_map/ppermute | solution.py:19
  126.2 1.3 collective-permute-start.5
  127.5 0.1 collective-permute-done.4
  127.6 4.2 %collective-permute-done.5 = bf16[1,64,128]{2,1,0:T(8,128)(2,1)S(1)} collective-permute-done((bf16[1,64,128]{2,1,0:T(8,128)(2,1)S(1)}, bf16[1,64,128]{2,1,0:T(8,128)(2,1)S(1)}, u32[]{:S(2)}, u32[]{:S(2)}) %collective-permute-start.5) | collective-permute-done | bytes 16416 | tf_op jit(solution)/shard_map/ppermute | solution.py:22
  131.8 1.9 collective-permute-start.6
  133.7 3.6 %collective-permute-start.7 = (bf16[1,80,128]{2,1,0:T(8,128)(2,1)S(1)}, bf16[1,80,128]{2,1,0:T(8,128)(2,1)S(1)}, u32[]{:S(2)}, u32[]{:S(2)}) collective-permute-start(bf16[1,80,128]{2,1,0:T(8,128)(2,1)S(1)} %maximum_bitcast_fusion.3), channel_id=1, source_target_pairs={{8,0},{16,8},{24,16},{32,24},{40,32},{48,40},{56,48},{64,56},{72,6... | collective-permute-start | bytes 61448 | tf_op jit(solution)/shard_map/ppermute | solution.py:22
  137.4 0.0 collective-permute-done.6
  137.4 1.4 collective-permute-done.7
  138.9 28.4 %gather_fusion.3 = bf16[13824,128]{1,0:T(8,128)(2,1)} fusion(bf16[801,128]{1,0:T(8,128)(2,1)S(1)} %constant_dynamic-update-slice_fusion.10, s32[14336]{0:T(1024)S(1)} %pad_clamp_fusion), kind=kCustom, calls=%fused_computation.1.clone | custom fusion | bytes 7133184 | tf_op jit(solution)/shard_map/jit(_take)/gather | solution.py:65
  167.3 6.6 %reshape.129 = bf16[512,27,128]{2,1,0:T(8,128)(2,1)} reshape(bf16[13824,128]{1,0:T(8,128)(2,1)} %gather_fusion.3) | data formatting | bytes 7077888 | tf_op jit(solution)/shard_map/jit(_take)/gather | solution.py:65
  173.9 0.0 copy-start.6
  173.9 10.1 %broadcast_select_fusion.1 = bf16[512,27,128]{2,1,0:T(8,128)(2,1)S(1)} fusion(bf16[512,27,128]{2,1,0:T(8,128)(2,1)} %reshape.129, pred[512,27]{1,0:T(8,128)(4,1)S(1)} %copy.13), kind=kLoop, calls=%fused_computation.5 | loop fusion | flops 1769472 | bytes 7091712 | tf_op jit(solution)/shard_map/jit(_take)/select_n | solution.py:65
  184.0 0.0 copy-done.6
  184.1 0.0 copy-start.1
  184.1 0.0 copy-start.4
  184.1 0.0 copy-start.5
  184.1 1.2 multiply_reduce_fusion
  185.3 14.2 %all-reduce.2 = (f32[128]{0:T(128)S(1)}, f32[128]{0:T(128)S(1)}) all-reduce(f32[128]{0:T(128)S(1)} %get-tuple-element.7, f32[128]{0:T(128)S(1)} %get-tuple-element.6), channel_id=1, replica_groups=mesh['slab_0'=8,'slab_1'=4,'slab_2'=2,'tile'=8] {'slab_0'}, use_global_device_ids=true, to_apply=%region_15.17 | all-reduce | flops 256 | bytes 2048 | tf_op jit(solution)/shard_map/psum | solution.py:29
  199.5 10.2 %all-reduce.4 = (f32[128]{0:T(128)S(1)}, f32[128]{0:T(128)S(1)}) all-reduce(f32[128]{0:T(128)S(1)} %get-tuple-element.15, f32[128]{0:T(128)S(1)} %get-tuple-element.16), channel_id=1, replica_groups=mesh['slab_0'=8,'slab_1'=4,'slab_2'=2,'tile'=8] {'slab_1'}, use_global_device_ids=true, to_apply=%region_16.18 | all-reduce | flops 256 | bytes 2048 | tf_op jit(solution)/shard_map/psum | solution.py:29
  209.7 2.5 %all-reduce.6 = (f32[128]{0:T(128)S(1)}, f32[128]{0:T(128)S(1)}) all-reduce(f32[128]{0:T(128)S(1)} %get-tuple-element.20, f32[128]{0:T(128)S(1)} %get-tuple-element.21), channel_id=1, replica_groups=mesh['slab_0'=8,'slab_1'=4,'slab_2'=2,'tile'=8] {'slab_2'}, use_global_device_ids=true, to_apply=%region_17.19 | all-reduce | flops 256 | bytes 2048 | tf_op jit(solution)/shard_map/psum | solution.py:29
  212.2 17.6 %all-reduce = (f32[128]{0:T(128)S(1)}, f32[128]{0:T(128)S(1)}) all-reduce(f32[128]{0:T(128)S(1)} %get-tuple-element.25, f32[128]{0:T(128)S(1)} %get-tuple-element.26), channel_id=1, replica_groups=mesh['slab_0'=8,'slab_1'=4,'slab_2'=2,'tile'=8] {'tile'}, use_global_device_ids=true, to_apply=%region_18.20 | all-reduce | flops 256 | bytes 2048 | tf_op jit(solution)/shard_map/psum | solution.py:29
  229.8 0.7 add_rsqrt_fusion
  230.4 0.0 copy-done.1
  230.4 0.0 copy-done.4
  230.4 0.0 copy-done.5
  230.4 0.8 fusion.10
  (31 shorter events, 0.2 us)
Async XLA Ops:
  0.0 63.8 %copy-start = (bf16[27,128,128]{2,1,0:T(8,128)(2,1)S(1)}, bf16[27,128,128]{2,1,0:T(8,128)(2,1)}, u32[]{:S(2)}) copy-start(bf16[27,128,128]{2,1,0:T(8,128)(2,1)} %param.16) | copy-start | bytes 2654212
  2.5 8.6 %collective-permute-start = (bf16[1,64,128]{2,1,0:T(8,128)(2,1)S(1)}, bf16[1,64,128]{2,1,0:T(8,128)(2,1)S(1)}, u32[]{:S(2)}, u32[]{:S(2)}) collective-permute-start(bf16[1,64,128]{2,1,0:T(8,128)(2,1)S(1)} %get-tuple-element.42), channel_id=1, source_target_pairs={{0,1},{1,2},{2,3},{3,4},{4,5},{5,6},{6,7},{8,9},{9,10},{10,11},{11... | collective-permute-start | bytes 49160 | tf_op jit(solution)/shard_map/ppermute | solution.py:19
  6.0 5.6 %collective-permute-start.1 = (bf16[1,64,128]{2,1,0:T(8,128)(2,1)S(1)}, bf16[1,64,128]{2,1,0:T(8,128)(2,1)S(1)}, u32[]{:S(2)}, u32[]{:S(2)}) collective-permute-start(bf16[1,64,128]{2,1,0:T(8,128)(2,1)S(1)} %get-tuple-element.41), channel_id=1, source_target_pairs={{1,0},{2,1},{3,2},{4,3},{5,4},{6,5},{7,6},{9,8},{10,9},{11,10},{12... | collective-permute-start | bytes 49160 | tf_op jit(solution)/shard_map/ppermute | solution.py:22
  11.6 5.6 %collective-permute-start.2 = (bf16[1,80,128]{2,1,0:T(8,128)(2,1)S(1)}, bf16[1,80,128]{2,1,0:T(8,128)(2,1)S(1)}, u32[]{:S(2)}, u32[]{:S(2)}) collective-permute-start(bf16[1,80,128]{2,1,0:T(8,128)(2,1)S(1)} %maximum_bitcast_fusion), channel_id=1, source_target_pairs={{0,8},{8,16},{16,24},{24,32},{32,40},{40,48},{48,56},{56,64},{64,7... | collective-permute-start | bytes 61448 | tf_op jit(solution)/shard_map/ppermute | solution.py:19
  13.6 5.1 %collective-permute-start.3 = (bf16[1,80,128]{2,1,0:T(8,128)(2,1)S(1)}, bf16[1,80,128]{2,1,0:T(8,128)(2,1)S(1)}, u32[]{:S(2)}, u32[]{:S(2)}) collective-permute-start(bf16[1,80,128]{2,1,0:T(8,128)(2,1)S(1)} %maximum_bitcast_fusion.1), channel_id=1, source_target_pairs={{8,0},{16,8},{24,16},{32,24},{40,32},{48,40},{56,48},{64,56},{72,6... | collective-permute-start | bytes 61448 | tf_op jit(solution)/shard_map/ppermute | solution.py:22
  63.8 58.6 %copy-start.2 = (f32[128]{0:T(128)S(1)}, f32[128]{0:T(128)}, u32[]{:S(2)}) copy-start(f32[128]{0:T(128)} %param.18) | copy-start | bytes 1540
  63.8 58.6 %copy-start.3 = (f32[128]{0:T(128)S(1)}, f32[128]{0:T(128)}, u32[]{:S(2)}) copy-start(f32[128]{0:T(128)} %param.17) | copy-start | bytes 1540
  123.4 4.2 %collective-permute-start.4 = (bf16[1,64,128]{2,1,0:T(8,128)(2,1)S(1)}, bf16[1,64,128]{2,1,0:T(8,128)(2,1)S(1)}, u32[]{:S(2)}, u32[]{:S(2)}) collective-permute-start(bf16[1,64,128]{2,1,0:T(8,128)(2,1)S(1)} %get-tuple-element.38), channel_id=1, source_target_pairs={{0,1},{1,2},{2,3},{3,4},{4,5},{5,6},{6,7},{8,9},{9,10},{10,11},{11... | collective-permute-start | bytes 49160 | tf_op jit(solution)/shard_map/ppermute | solution.py:19
  126.2 5.6 %collective-permute-start.5 = (bf16[1,64,128]{2,1,0:T(8,128)(2,1)S(1)}, bf16[1,64,128]{2,1,0:T(8,128)(2,1)S(1)}, u32[]{:S(2)}, u32[]{:S(2)}) collective-permute-start(bf16[1,64,128]{2,1,0:T(8,128)(2,1)S(1)} %get-tuple-element.37), channel_id=1, source_target_pairs={{1,0},{2,1},{3,2},{4,3},{5,4},{6,5},{7,6},{9,8},{10,9},{11,10},{12... | collective-permute-start | bytes 49160 | tf_op jit(solution)/shard_map/ppermute | solution.py:22
  131.8 5.6 %collective-permute-start.6 = (bf16[1,80,128]{2,1,0:T(8,128)(2,1)S(1)}, bf16[1,80,128]{2,1,0:T(8,128)(2,1)S(1)}, u32[]{:S(2)}, u32[]{:S(2)}) collective-permute-start(bf16[1,80,128]{2,1,0:T(8,128)(2,1)S(1)} %maximum_bitcast_fusion.2), channel_id=1, source_target_pairs={{0,8},{8,16},{16,24},{24,32},{32,40},{40,48},{48,56},{56,64},{64,7... | collective-permute-start | bytes 61448 | tf_op jit(solution)/shard_map/ppermute | solution.py:19
  133.7 5.1 %collective-permute-start.7 = (bf16[1,80,128]{2,1,0:T(8,128)(2,1)S(1)}, bf16[1,80,128]{2,1,0:T(8,128)(2,1)S(1)}, u32[]{:S(2)}, u32[]{:S(2)}) collective-permute-start(bf16[1,80,128]{2,1,0:T(8,128)(2,1)S(1)} %maximum_bitcast_fusion.3), channel_id=1, source_target_pairs={{8,0},{16,8},{24,16},{32,24},{40,32},{48,40},{56,48},{64,56},{72,6... | collective-permute-start | bytes 61448 | tf_op jit(solution)/shard_map/ppermute | solution.py:22
  173.9 10.2 %copy-start.6 = (bf16[27,128,128]{2,1,0:T(8,128)(2,1)S(1)}, bf16[27,128,128]{2,1,0:T(8,128)(2,1)}, u32[]{:S(2)}) copy-start(bf16[27,128,128]{2,1,0:T(8,128)(2,1)} %param.19) | copy-start | bytes 2654212
  184.1 46.4 %copy-start.1 = (bf16[1,1,512,128]{3,2,1,0:T(8,128)(2,1)S(1)}, bf16[1,1,512,128]{3,2,1,0:T(8,128)(2,1)}, u32[]{:S(2)}) copy-start(bf16[1,1,512,128]{3,2,1,0:T(8,128)(2,1)} %param.12) | copy-start | bytes 393220
  184.1 46.4 %copy-start.4 = (f32[128]{0:T(128)S(1)}, f32[128]{0:T(128)}, u32[]{:S(2)}) copy-start(f32[128]{0:T(128)} %param.21) | copy-start | bytes 1540
  184.1 46.4 %copy-start.5 = (f32[128]{0:T(128)S(1)}, f32[128]{0:T(128)}, u32[]{:S(2)}) copy-start(f32[128]{0:T(128)} %param.20) | copy-start | bytes 1540
where the time goes:
time: 233 us; the launch traced here: 231 us
  blocking collectives  101 us (43%)
  local copies, waits for them, and re-layouts  74.2 us (32%)
  other arithmetic  24.9 us (11%)
  starting transfers between devices  19.9 us (9%)
  waiting for transfers between devices  7.7 us (3%)
  matrix products  2.55 us (1%)
    psum x8, blocking collectives, by_axis(): shard = lax.psum(shard, axis)  101 us
    gather x4, local copies, waits for them, and re-layouts, pick_rows(): gathered = jnp.take(lookup, tap_index.T, axis=0)  69.9 us
    select_n x3, other arithmetic, pick_rows(): gathered = jnp.take(lookup, tap_index.T, axis=0)  21 us
    ppermute x4, starting transfers between devices, extended(): lax.ppermute(lax.slice_in_dim(block, block.shape[dim] - width, None, axis...  10 us
    ppermute x4, starting transfers between devices, extended(): lax.ppermute(lax.slice_in_dim(block, 0, width, axis=dim), axis, backward)  9.87 us
    ppermute x4, waiting for transfers between devices, extended(): lax.ppermute(lax.slice_in_dim(block, 0, width, axis=dim), axis, backward)  7.57 us
  transfers between devices with their start and end apart: 8, of which 5 were waited for; matrix products, arithmetic and copies ran while one was open for 1% of the time, Pallas kernels for 0%

commit v1 on v0

--- a/solution.py
+++ b/solution.py
@@ -26,7 +26,8 @@
 
 def by_axis(shard, axes):
     for axis in axes:
-        shard = lax.psum(shard, axis)
+        parts = lax.all_gather(shard, axis, axis=0, tiled=False)
+        shard = parts.sum(axis=0)
     return shard
 
 

time: 233 us -> 358 us (1.54)
  the two profiles are of different devices: /device:TPU:2 before, /device:TPU:24 now
where the time goes in v1:
time: 358 us; the launch traced here: 356 us
  blocking collectives  215 us (60%)
  local copies, waits for them, and re-layouts  84 us (23%)
  other arithmetic  27.9 us (8%)
  starting transfers between devices  17.6 us (5%)
  waiting for transfers between devices  7.89 us (2%)
    all_gather x16, blocking collectives, by_axis(): parts = lax.all_gather(shard, axis, axis=0, tiled=False)  163 us
    gather x4, local copies, waits for them, and re-layouts, pick_rows(): gathered = jnp.take(lookup, tap_index.T, axis=0)  69.9 us
    unnamed x4, blocking collectives  52.2 us
    select_n x3, other arithmetic, pick_rows(): gathered = jnp.take(lookup, tap_index.T, axis=0)  21 us
    unnamed x43, local copies, waits for them, and re-layouts  10.9 us
    ppermute x4, starting transfers between devices, extended(): lax.ppermute(lax.slice_in_dim(block, block.shape[dim] - width, None, axis...  10.4 us
    ppermute x4, waiting for transfers between devices, extended(): lax.ppermute(lax.slice_in_dim(block, 0, width, axis=dim), axis, backward)  7.88 us
    ppermute x4, starting transfers between devices, extended(): lax.ppermute(lax.slice_in_dim(block, 0, width, axis=dim), axis, backward)  7.21 us
  transfers between devices with their start and end apart: 8, of which 3 were waited for; matrix products, arithmetic and copies ran while one was open for 4% of the time, Pallas kernels for 0%

profile of v1, /device:TPU:24, one launch (start us, length us, event | category | flops | bytes accessed | tf_op | source)
XLA Modules:
  0.0 356.2 jit_solution(18365566848309902229)
XLA Ops:
  0.0 0.8 compare_select_fusion.1
  0.9 1.6 gather_fusion
  2.5 4.7 %collective-permute-start = (bf16[1,64,128]{2,1,0:T(8,128)(2,1)S(1)}, bf16[1,64,128]{2,1,0:T(8,128)(2,1)S(1)}, u32[]{:S(2)}, u32[]{:S(2)}) collective-permute-start(bf16[1,64,128]{2,1,0:T(8,128)(2,1)S(1)} %get-tuple-element.22), channel_id=1, source_target_pairs={{0,1},{1,2},{2,3},{3,4},{4,5},{5,6},{6,7},{8,9},{9,10},{10,11},{11... | collective-permute-start | bytes 49160 | tf_op jit(solution)/shard_map/ppermute | solution.py:19
  7.2 1.9 collective-permute-start.1
  9.1 0.9 constant_dynamic-update-slice_fusion.9
  10.1 0.8 compare_select_fusion
  10.9 0.8 compare_and_fusion
  11.7 0.1 copy.21
  11.9 0.2 reshape.226
  12.8 1.3 dynamic-slice
  14.1 0.7 dynamic-update-slice
  14.7 23.2 %all-reduce = f32[8]{0:T(128)S(1)} all-reduce(f32[8]{0:T(128)S(1)} %dynamic-update-slice), channel_id=1, replica_groups=mesh['slab_0'=8,'slab_1'=4,'slab_2'=2,'tile'=8] {'slab_0'}, use_global_device_ids=true, to_apply=%add | all-reduce | flops 8 | bytes 64
  37.9 1.3 dynamic-slice.1
  39.1 0.7 reduce_sum.237
  39.8 1.4 dynamic-update-slice.1
  41.2 10.5 %all-reduce.1 = f32[4]{0:T(128)S(1)} all-reduce(f32[4]{0:T(128)S(1)} %dynamic-update-slice.1), channel_id=1, replica_groups=mesh['slab_0'=8,'slab_1'=4,'slab_2'=2,'tile'=8] {'slab_1'}, use_global_device_ids=true, to_apply=%add.1 | all-reduce | flops 4 | bytes 32
  51.6 1.3 dynamic-slice.2
  52.9 0.7 reduce_sum.238
  53.6 1.4 dynamic-update-slice.2
  54.9 2.4 all-reduce.2
  57.4 1.3 dynamic-slice.3
  58.6 0.7 reduce_sum.239
  59.3 1.4 dynamic-update-slice.3
  60.7 16.1 %all-reduce.3 = f32[8]{0:T(128)S(1)} all-reduce(f32[8]{0:T(128)S(1)} %dynamic-update-slice.3), channel_id=1, replica_groups=mesh['slab_0'=8,'slab_1'=4,'slab_2'=2,'tile'=8] {'tile'}, use_global_device_ids=true, to_apply=%add.3 | all-reduce | flops 8 | bytes 64
  76.8 0.2 copy.19
  77.0 0.6 reduce_sum.240
  77.6 1.3 collective-permute-start.2
  79.0 1.3 collective-permute-start.3
  80.3 1.8 collective-permute-done.3
  82.1 28.4 %gather_fusion.2 = bf16[13824,128]{1,0:T(8,128)(2,1)} fusion(bf16[801,128]{1,0:T(8,128)(2,1)S(1)} %constant_dynamic-update-slice_fusion, s32[14336]{0:T(1024)S(1)} %pad_clamp_fusion), kind=kCustom, calls=%fused_computation.clone | custom fusion | bytes 7133184 | tf_op jit(solution)/shard_map/jit(_take)/gather | solution.py:66
  110.5 6.6 %reshape.229 = bf16[512,27,128]{2,1,0:T(8,128)(2,1)} reshape(bf16[13824,128]{1,0:T(8,128)(2,1)} %gather_fusion.2) | data formatting | bytes 7077888 | tf_op jit(solution)/shard_map/jit(_take)/gather | solution.py:66
  117.1 10.1 %broadcast_select_fusion = bf16[512,27,128]{2,1,0:T(8,128)(2,1)S(1)} fusion(bf16[512,27,128]{2,1,0:T(8,128)(2,1)} %reshape.229, pred[512,27]{1,0:T(8,128)(4,1)S(1)} %copy.19), kind=kLoop, calls=%fused_computation.4 | loop fusion | flops 1769472 | bytes 7091712 | tf_op jit(solution)/shard_map/jit(_take)/select_n | solution.py:66
  127.2 1.3 multiply_reduce_fusion.2
  128.5 17.8 %all-gather.16 = f32[8,1,128]{2,1,0:T(1,128)S(1)} all-gather(f32[1,1,128]{2,1,0:T(1,128)S(1)} %bitcast.147), channel_id=2, replica_groups=mesh['slab_0'=8,'slab_1'=4,'slab_2'=2,'tile'=8] {'slab_0'}, dimensions={0}, use_global_device_ids=true | all-gather | bytes 4608 | tf_op jit(solution)/shard_map/all_gather | solution.py:29
  146.3 7.0 %all-gather.17 = f32[4,1,128]{2,1,0:T(1,128)S(1)} all-gather(f32[1,1,128]{2,1,0:T(1,128)S(1)} %bitcast.137), channel_id=3, replica_groups=mesh['slab_0'=8,'slab_1'=4,'slab_2'=2,'tile'=8] {'slab_1'}, dimensions={0}, use_global_device_ids=true | all-gather | bytes 2560 | tf_op jit(solution)/shard_map/all_gather | solution.py:29
  153.3 1.8 all-gather.18
  155.1 13.3 %all-gather.19 = f32[8,1,128]{2,1,0:T(1,128)S(1)} all-gather(f32[1,1,128]{2,1,0:T(1,128)S(1)} %bitcast.141), channel_id=5, replica_groups=mesh['slab_0'=8,'slab_1'=4,'slab_2'=2,'tile'=8] {'tile'}, dimensions={0}, use_global_device_ids=true | all-gather | bytes 4608 | tf_op jit(solution)/shard_map/all_gather | solution.py:29
  168.4 14.6 %all-gather.20 = f32[8,1,128]{2,1,0:T(1,128)S(1)} all-gather(f32[1,1,128]{2,1,0:T(1,128)S(1)} %bitcast.145), channel_id=6, replica_groups=mesh['slab_0'=8,'slab_1'=4,'slab_2'=2,'tile'=8] {'slab_0'}, dimensions={0}, use_global_device_ids=true | all-gather | bytes 4608 | tf_op jit(solution)/shard_map/all_gather | solution.py:29
  183.1 9.0 %all-gather.21 = f32[4,1,128]{2,1,0:T(1,128)S(1)} all-gather(f32[1,1,128]{2,1,0:T(1,128)S(1)} %bitcast.138), channel_id=7, replica_groups=mesh['slab_0'=8,'slab_1'=4,'slab_2'=2,'tile'=8] {'slab_1'}, dimensions={0}, use_global_device_ids=true | all-gather | bytes 2560 | tf_op jit(solution)/shard_map/all_gather | solution.py:29
  192.1 1.8 all-gather.22
  193.9 15.3 %all-gather.23 = f32[8,1,128]{2,1,0:T(1,128)S(1)} all-gather(f32[1,1,128]{2,1,0:T(1,128)S(1)} %bitcast.142), channel_id=9, replica_groups=mesh['slab_0'=8,'slab_1'=4,'slab_2'=2,'tile'=8] {'tile'}, dimensions={0}, use_global_device_ids=true | all-gather | bytes 4608 | tf_op jit(solution)/shard_map/all_gather | solution.py:29
  209.3 0.7 add_rsqrt_fusion.1
  210.0 0.1 constant_dynamic-update-slice_fusion.19
  210.1 0.9 gather_fusion.1
  211.0 3.1 collective-permute-start.4
  214.1 2.7 collective-permute-start.5
  216.8 4.1 %collective-permute-done.5 = bf16[1,64,128]{2,1,0:T(8,128)(2,1)S(1)} collective-permute-done((bf16[1,64,128]{2,1,0:T(8,128)(2,1)S(1)}, bf16[1,64,128]{2,1,0:T(8,128)(2,1)S(1)}, u32[]{:S(2)}, u32[]{:S(2)}) %collective-permute-start.5) | collective-permute-done | bytes 16416 | tf_op jit(solution)/shard_map/ppermute | solution.py:22
  221.0 1.3 collective-permute-start.6
  222.3 1.3 collective-permute-start.7
  223.6 2.0 collective-permute-done.7
  225.7 28.4 %gather_fusion.3 = bf16[13824,128]{1,0:T(8,128)(2,1)} fusion(bf16[801,128]{1,0:T(8,128)(2,1)S(1)} %constant_dynamic-update-slice_fusion.10, s32[14336]{0:T(1024)S(1)} %pad_clamp_fusion), kind=kCustom, calls=%fused_computation.1.clone | custom fusion | bytes 7133184 | tf_op jit(solution)/shard_map/jit(_take)/gather | solution.py:66
  254.0 6.6 %reshape.233 = bf16[512,27,128]{2,1,0:T(8,128)(2,1)} reshape(bf16[13824,128]{1,0:T(8,128)(2,1)} %gather_fusion.3) | data formatting | bytes 7077888 | tf_op jit(solution)/shard_map/jit(_take)/gather | solution.py:66
  260.6 10.1 %broadcast_select_fusion.1 = bf16[512,27,128]{2,1,0:T(8,128)(2,1)S(1)} fusion(bf16[512,27,128]{2,1,0:T(8,128)(2,1)} %reshape.233, pred[512,27]{1,0:T(8,128)(4,1)S(1)} %copy.19), kind=kLoop, calls=%fused_computation.5 | loop fusion | flops 1769472 | bytes 7091712 | tf_op jit(solution)/shard_map/jit(_take)/select_n | solution.py:66
  270.8 1.2 multiply_reduce_fusion
  272.1 18.5 %all-gather.24 = f32[8,1,128]{2,1,0:T(1,128)S(1)} all-gather(f32[1,1,128]{2,1,0:T(1,128)S(1)} %bitcast.148), channel_id=10, replica_groups=mesh['slab_0'=8,'slab_1'=4,'slab_2'=2,'tile'=8] {'slab_0'}, dimensions={0}, use_global_device_ids=true | all-gather | bytes 4608 | tf_op jit(solution)/shard_map/all_gather | solution.py:29
  290.6 7.0 %all-gather.25 = f32[4,1,128]{2,1,0:T(1,128)S(1)} all-gather(f32[1,1,128]{2,1,0:T(1,128)S(1)} %bitcast.139), channel_id=11, replica_groups=mesh['slab_0'=8,'slab_1'=4,'slab_2'=2,'tile'=8] {'slab_1'}, dimensions={0}, use_global_device_ids=true | all-gather | bytes 2560 | tf_op jit(solution)/shard_map/all_gather | solution.py:29
  297.6 1.8 all-gather.26
  299.4 13.0 %all-gather.27 = f32[8,1,128]{2,1,0:T(1,128)S(1)} all-gather(f32[1,1,128]{2,1,0:T(1,128)S(1)} %bitcast.143), channel_id=13, replica_groups=mesh['slab_0'=8,'slab_1'=4,'slab_2'=2,'tile'=8] {'tile'}, dimensions={0}, use_global_device_ids=true | all-gather | bytes 4608 | tf_op jit(solution)/shard_map/all_gather | solution.py:29
  312.4 15.9 %all-gather.28 = f32[8,1,128]{2,1,0:T(1,128)S(1)} all-gather(f32[1,1,128]{2,1,0:T(1,128)S(1)} %bitcast.146), channel_id=14, replica_groups=mesh['slab_0'=8,'slab_1'=4,'slab_2'=2,'tile'=8] {'slab_0'}, dimensions={0}, use_global_device_ids=true | all-gather | bytes 4608 | tf_op jit(solution)/shard_map/all_gather | solution.py:29
  328.3 9.0 %all-gather.29 = f32[4,1,128]{2,1,0:T(1,128)S(1)} all-gather(f32[1,1,128]{2,1,0:T(1,128)S(1)} %bitcast.140), channel_id=15, replica_groups=mesh['slab_0'=8,'slab_1'=4,'slab_2'=2,'tile'=8] {'slab_1'}, dimensions={0}, use_global_device_ids=true | all-gather | bytes 2560 | tf_op jit(solution)/shard_map/all_gather | solution.py:29
  337.3 1.8 all-gather.30
  339.1 15.6 %all-gather.31 = f32[8,1,128]{2,1,0:T(1,128)S(1)} all-gather(f32[1,1,128]{2,1,0:T(1,128)S(1)} %bitcast.144), channel_id=17, replica_groups=mesh['slab_0'=8,'slab_1'=4,'slab_2'=2,'tile'=8] {'tile'}, dimensions={0}, use_global_device_ids=true | all-gather | bytes 4608 | tf_op jit(solution)/shard_map/all_gather | solution.py:29
  354.7 0.7 add_rsqrt_fusion
  355.4 0.8 fusion.10
  (71 shorter events, 0.7 us)
Async XLA Ops:
  0.0 127.2 %copy-start = (bf16[27,128,128]{2,1,0:T(8,128)(2,1)S(1)}, bf16[27,128,128]{2,1,0:T(8,128)(2,1)}, u32[]{:S(2)}) copy-start(bf16[27,128,128]{2,1,0:T(8,128)(2,1)} %param.16) | copy-start | bytes 2654212
  2.5 75.1 %collective-permute-start = (bf16[1,64,128]{2,1,0:T(8,128)(2,1)S(1)}, bf16[1,64,128]{2,1,0:T(8,128)(2,1)S(1)}, u32[]{:S(2)}, u32[]{:S(2)}) collective-permute-start(bf16[1,64,128]{2,1,0:T(8,128)(2,1)S(1)} %get-tuple-element.22), channel_id=1, source_target_pairs={{0,1},{1,2},{2,3},{3,4},{4,5},{5,6},{6,7},{8,9},{9,10},{10,11},{11... | collective-permute-start | bytes 49160 | tf_op jit(solution)/shard_map/ppermute | solution.py:19
  7.2 70.4 %collective-permute-start.1 = (bf16[1,64,128]{2,1,0:T(8,128)(2,1)S(1)}, bf16[1,64,128]{2,1,0:T(8,128)(2,1)S(1)}, u32[]{:S(2)}, u32[]{:S(2)}) collective-permute-start(bf16[1,64,128]{2,1,0:T(8,128)(2,1)S(1)} %get-tuple-element.21), channel_id=1, source_target_pairs={{1,0},{2,1},{3,2},{4,3},{5,4},{6,5},{7,6},{9,8},{10,9},{11,10},{12... | collective-permute-start | bytes 49160 | tf_op jit(solution)/shard_map/ppermute | solution.py:22
  77.6 2.6 collective-permute-start.2
  79.0 3.1 collective-permute-start.3
  127.2 82.8 %copy-start.2 = (f32[128]{0:T(128)S(1)}, f32[128]{0:T(128)}, u32[]{:S(2)}) copy-start(f32[128]{0:T(128)} %param.18) | copy-start | bytes 1540
  127.2 82.8 %copy-start.3 = (f32[128]{0:T(128)S(1)}, f32[128]{0:T(128)}, u32[]{:S(2)}) copy-start(f32[128]{0:T(128)} %param.17) | copy-start | bytes 1540
  211.0 5.9 %collective-permute-start.4 = (bf16[1,64,128]{2,1,0:T(8,128)(2,1)S(1)}, bf16[1,64,128]{2,1,0:T(8,128)(2,1)S(1)}, u32[]{:S(2)}, u32[]{:S(2)}) collective-permute-start(bf16[1,64,128]{2,1,0:T(8,128)(2,1)S(1)} %get-tuple-element.18), channel_id=1, source_target_pairs={{0,1},{1,2},{2,3},{3,4},{4,5},{5,6},{6,7},{8,9},{9,10},{10,11},{11... | collective-permute-start | bytes 49160 | tf_op jit(solution)/shard_map/ppermute | solution.py:19
  214.1 6.8 %collective-permute-start.5 = (bf16[1,64,128]{2,1,0:T(8,128)(2,1)S(1)}, bf16[1,64,128]{2,1,0:T(8,128)(2,1)S(1)}, u32[]{:S(2)}, u32[]{:S(2)}) collective-permute-start(bf16[1,64,128]{2,1,0:T(8,128)(2,1)S(1)} %get-tuple-element.17), channel_id=1, source_target_pairs={{1,0},{2,1},{3,2},{4,3},{5,4},{6,5},{7,6},{9,8},{10,9},{11,10},{12... | collective-permute-start | bytes 49160 | tf_op jit(solution)/shard_map/ppermute | solution.py:22
  221.0 2.6 collective-permute-start.6
  222.3 3.3 collective-permute-start.7
  260.6 10.2 %copy-start.6 = (bf16[27,128,128]{2,1,0:T(8,128)(2,1)S(1)}, bf16[27,128,128]{2,1,0:T(8,128)(2,1)}, u32[]{:S(2)}) copy-start(bf16[27,128,128]{2,1,0:T(8,128)(2,1)} %param.19) | copy-start | bytes 2654212
  270.8 84.6 %copy-start.1 = (bf16[1,1,512,128]{3,2,1,0:T(8,128)(2,1)S(1)}, bf16[1,1,512,128]{3,2,1,0:T(8,128)(2,1)}, u32[]{:S(2)}) copy-start(bf16[1,1,512,128]{3,2,1,0:T(8,128)(2,1)} %param.12) | copy-start | bytes 393220
  270.8 84.6 %copy-start.4 = (f32[128]{0:T(128)S(1)}, f32[128]{0:T(128)}, u32[]{:S(2)}) copy-start(f32[128]{0:T(128)} %param.21) | copy-start | bytes 1540
  270.8 84.6 %copy-start.5 = (f32[128]{0:T(128)S(1)}, f32[128]{0:T(128)}, u32[]{:S(2)}) copy-start(f32[128]{0:T(128)} %param.20) | copy-start | bytes 1540
